TPU v7x, 32 devices: a whole 2x2x4 slice. The times are simulated.
32 devices in a mesh: group: 2 (over x), tile: 16 (over z, y, core).
Axes of the slice: x: 2, y: 2, z: 4, core: 2. Of those that a mesh axis runs over, the one named last changes fastest.
Arguments:
- hadamard: int32 [128, 1152], P(None, 'tile'), may hold values from -1 to 1, as said below
- stroke: float32 [2304], P(('group', 'tile')), parts along dimension 0, may hold values from 0.3 to 1
- influence: bfloat16 [3, 2304, 8192], P(None, ('group', 'tile')), parts along dimension 1, may hold values from -0.4375 to 0.4375
- amplitude: float32 [1024, 16, 16], P(('group', 'tile')), parts along dimension 0, may hold values from 0.3 to 1
- aberration: float32 [1024, 16, 16], P(('group', 'tile')), parts along dimension 0, may hold values from -3 to 3
- valid_mask: int32 [1024], P(('group', 'tile')), parts along dimension 0, may hold values from 0 to 1, as said below
Outputs:
- imat: float32 [2304, 2, 512], P(('group', 'tile')), parts along dimension 0
There are 2 independent parts, one for each index of `group`. A program takes and returns all parts, laid end to end along the dimension named above; an argument that names none is the same for every part. Nothing has to cross between parts.
Inputs may be any that keep to these rules, and one draw needn't show every extreme that they name: `hadamard`: each column is one column of a Sylvester-Hadamard matrix whose order is the least power of two not below 1152, restricted to 128 distinct rows of it; different actuators take different columns. `valid_mask`: every pupil tile of 32 subapertures holds at least one valid subaperture.
All inputs are finite; a program needn't handle non-finite values.
Results may differ from a plain program's by a relative error of at most 0.0055.
Values may be sent and summed in bfloat16 or wider, within the bound.
A program may use at most 128 MiB of HBM per device.

v0:
```python
import math
import jax
import jax.numpy as jnp
from jax import lax
from jax.sharding import PartitionSpec as P

PIX = 16
HIGHEST = lax.Precision.HIGHEST


def passed_along(value, axis, steps):
    count = lax.axis_size(axis)
    first, last = (max(0, -steps), min(count, count - steps))
    return lax.ppermute(value, axis, [(source, source + steps) for source in range(first, last)])


def shortened(x):
    return jax.tree.map(lambda a: a.astype(jnp.bfloat16) if a.dtype == jnp.float32 else a, x)


def transform_tables(samples, pixels):
    freqs = jnp.arange(pixels, dtype=jnp.float32) - pixels / 2.0
    places = jnp.arange(samples, dtype=jnp.float32)
    angle = 2.0 * jnp.pi * freqs[:, None] * places[None, :] / (2.0 * samples)
    return (jnp.cos(angle), -jnp.sin(angle))


def kron_tables(samples, pixels):
    table_real, table_imag = transform_tables(samples, pixels)
    kron_real = jnp.kron(table_real, table_real) - jnp.kron(table_imag, table_imag)
    kron_imag = jnp.kron(table_real, table_imag) + jnp.kron(table_imag, table_real)
    upper = jnp.concatenate([kron_real.T, kron_imag.T], axis=1)
    lower = jnp.concatenate([-kron_imag.T, kron_real.T], axis=1)
    transform = jnp.concatenate([upper, lower], axis=0)
    centre = jnp.arange(pixels, dtype=jnp.float32) - (pixels - 1) / 2.0
    along_u = jnp.repeat(centre, pixels)
    along_v = jnp.tile(centre, pixels)
    moments = jnp.stack([jnp.ones_like(along_u), along_u, along_v], axis=1)
    return (transform, moments)


def spot_slopes(phase_map, amplitude, aberration, valid_mask):
    patterns, sub_count, samples = (phase_map.shape[0], phase_map.shape[1], phase_map.shape[2])
    flat = samples * samples
    transform, moments = kron_tables(samples, PIX)
    half = PIX * PIX
    phase_rows = phase_map.reshape(patterns, sub_count, flat)
    amp_rows = amplitude.reshape(sub_count, flat)[None]
    abe_rows = aberration.reshape(sub_count, flat)[None]
    results = []
    for pattern_sign in (1.0, -1.0):
        angles = abe_rows + pattern_sign * phase_rows
        field = jnp.concatenate([amp_rows * jnp.cos(angles), amp_rows * jnp.sin(angles)], axis=2)
        focal = jnp.dot(field.reshape(patterns * sub_count, 2 * flat), transform, precision=HIGHEST)
        intensity = focal[:, :half] * focal[:, :half] + focal[:, half:] * focal[:, half:]
        sums = jnp.dot(intensity, moments, precision=HIGHEST)
        centroid_x = sums[:, 1] / sums[:, 0]
        centroid_y = sums[:, 2] / sums[:, 0]
        results.append(
            jnp.stack([centroid_x, centroid_y], axis=1)
            .reshape(patterns, sub_count, 2)
            .transpose(0, 2, 1)
        )
    weights = valid_mask.astype(jnp.float32)[None, None, :]
    return ((results[0] - results[1]) * 0.5 * weights).astype(jnp.bfloat16)


def shape_term(commands, slab):
    term = jnp.dot(commands, slab, preferred_element_type=jnp.float32).astype(jnp.bfloat16)
    return lax.optimization_barrier(term)


def per_device(hadamard, stroke, influence, amplitude, aberration, valid_mask):
    patterns = hadamard.shape[0]
    sub_count = amplitude.shape[0]
    samples = amplitude.shape[1]
    commands = (stroke[None, :] * hadamard.astype(jnp.float32)).astype(jnp.bfloat16)
    local_term = shape_term(commands, influence[1])
    lower_cmds, lower_slab = passed_along((commands, influence[2]), "tile", 1)
    upper_cmds, upper_slab = passed_along((commands, influence[0]), "tile", -1)
    from_lower = shape_term(lower_cmds, lower_slab)
    from_upper = shape_term(upper_cmds, upper_slab)
    phase_map = (
        local_term.astype(jnp.float32)
        + from_lower.astype(jnp.float32)
        + from_upper.astype(jnp.float32)
    )
    block_rows = math.gcd(patterns, 64)
    blocks = phase_map.reshape(patterns // block_rows, block_rows, sub_count, samples, samples)

    def one_block(pattern_block):
        return spot_slopes(pattern_block, amplitude, aberration, valid_mask)

    slopes = lax.map(one_block, blocks).reshape(patterns, 2, sub_count)
    signs_half = hadamard.astype(jnp.bfloat16)
    summed = jnp.einsum(
        "pa,pcs->acs",
        signs_half,
        lax.all_gather(shortened(slopes), "tile", axis=2, tiled=True),
        preferred_element_type=jnp.float32,
    )
    return summed / (patterns * stroke)[:, None, None]


def solution(mesh):
    placed = (
        P(None, "tile"),
        P(("group", "tile")),
        P(None, ("group", "tile"), None),
        P(("group", "tile"), None, None),
        P(("group", "tile"), None, None),
        P(("group", "tile")),
    )
    return jax.shard_map(
        per_device,
        mesh=mesh,
        in_specs=placed,
        out_specs=P(("group", "tile"), None, None),
        check_vma=False,
    )
```

profile of v0, /device:TPU:0, one launch (start us, length us, event | category | flops | bytes accessed | tf_op | source)
XLA Modules:
  0.0 236.9 jit_solution(5249718799039673560)
XLA Ops:
  0.0 2.8 %slice_bitcast_fusion.1 = (bf16[72,8192]{1,0:T(8,128)(2,1)}, bf16[72,8192]{1,0:T(8,128)(2,1)S(1)}) fusion(bf16[3,72,8192]{2,1,0:T(8,128)(2,1)} %param.10), kind=kLoop, calls=%fused_computation.58 | loop fusion | bytes 4718592 | tf_op jit(solution)/shard_map/squeeze | solution.py:79
  2.8 3.6 %collective-permute-start.1 = (bf16[72,8192]{1,0:T(8,128)(2,1)}, bf16[72,8192]{1,0:T(8,128)(2,1)}, u32[]{:S(2)}, u32[]{:S(2)}) collective-permute-start(bf16[72,8192]{1,0:T(8,128)(2,1)} %get-tuple-element.136), channel_id=1, source_target_pairs={{0,1},{1,2},{2,3},{3,4},{4,5},{5,6},{6,7},{7,8},{8,9},{9,10},{10,1... | collective-permute-start | bytes 3538952 | tf_op jit(solution)/shard_map/ppermute | solution.py:14
  6.4 1.3 collective-permute-start.3
  7.7 0.1 multiply_convert_fusion
  7.8 4.1 %collective-permute-start = (bf16[128,72]{0,1:T(8,128)(2,1)S(1)}, bf16[128,72]{0,1:T(8,128)(2,1)S(1)}, u32[]{:S(2)}, u32[]{:S(2)}) collective-permute-start(bf16[128,72]{0,1:T(8,128)(2,1)S(1)} %multiply_convert_fusion), channel_id=1, source_target_pairs={{0,1},{1,2},{2,3},{3,4},{4,5},{5,6},{6,7},{7,8},{8,9},{9,10},{10,1... | collective-permute-start | bytes 55304 | tf_op jit(solution)/shard_map/ppermute | solution.py:14
  11.9 1.3 collective-permute-start.2
  13.2 2.0 convolution_convert_fusion.2
  15.3 2.0 convolution_convert_fusion.1
  17.3 2.0 convolution_convert_fusion
  19.3 2.8 %convert_add_fusion = f32[128,8192]{1,0:T(8,128)} fusion(bf16[128,8192]{1,0:T(8,128)(2,1)S(1)} %convolution_convert_fusion, bf16[128,8192]{1,0:T(8,128)(2,1)S(1)} %convolution_convert_fusion.1, bf16[128,8192]{1,0:T(8,128)(2,1)S(1)} %convolution_convert_fusion.2), kind=kLoop, calls=%fused_computation.55 | loop fusion | flops 5242880 | bytes 10485760 | tf_op jit(solution)/shard_map/add | solution.py:84
  22.1 5.6 %copy.28 = f32[128,8192]{0,1:T(8,128)} copy(f32[128,8192]{1,0:T(8,128)} %convert_add_fusion) | data formatting | bytes 8388608 | tf_op jit(solution)/shard_map/add | solution.py:84
  27.7 9.2 %reshape.211 = f32[2,64,32,16,16]{1,0,4,3,2:T(2,128)} reshape(f32[128,8192]{0,1:T(8,128)} %copy.28) | data formatting | bytes 8388608 | tf_op jit(solution)/shard_map/reshape | solution.py:89
  36.9 159.1 %while.12 = (s32[]{:T(128)}, bf16[2,64,2,32]{1,0,3,2:T(2,128)(2,1)S(1)}, f32[32,16,16]{0,2,1:T(8,128)S(1)}, f32[32,16,16]{0,2,1:T(8,128)S(1)}, f32[2,64,32,16,16...) while((s32[]{:T(128)}, ...), condition=%wide.region_1.2_spmd, body=%wide.region_0.1_spmd.sunk | while | flops 12933627904 | bytes 64969588 | solution.py:94
  36.9 9.7 %constant_dynamic-slice_fusion.2 = f32[1,64,32,16,16]{1,0,4,3,2:T(1,128)} fusion(f32[2,64,32,16,16]{1,0,4,3,2:T(2,128)} %get-tuple-element.223, s32[]{:T(128)} %get-tuple-element.209), kind=kLoop, calls=%fused_computation.46.clone.1 | loop fusion | bytes 4194308 | tf_op jit(solution)/shard_map/while/body/jit(dynamic_index_in_dim)/dynamic_slice | solution.py:94
  46.6 12.3 %copy.40 = f32[1,64,32,16,16]{2,1,4,3,0:T(8,128)} copy(f32[1,64,32,16,16]{1,0,4,3,2:T(1,128)} %constant_dynamic-slice_fusion.2) | data formatting | bytes 4194304 | tf_op jit(solution)/shard_map/while/body/jit(dynamic_index_in_dim)/dynamic_slice | solution.py:94
  58.9 7.5 %reshape.239 = f32[2048,256]{0,1:T(8,128)} reshape(f32[1,64,32,16,16]{2,1,4,3,0:T(8,128)} %copy.40) | data formatting | bytes 4194304 | tf_op jit(solution)/shard_map/while/body/eval_jaxpr/reshape | solution.py:47
  66.4 1.9 copy.41
  68.4 0.1 copy.43
  68.5 16.6 %bitcast_multiply_fusion.5 = (f32[2048,256]{1,0:T(8,128)}, f32[2048,256]{1,0:T(8,128)}, f32[2048,256]{1,0:T(8,128)}, f32[2048,256]{1,0:T(8,128)}) fusion(f32[2048,256]{1,0:T(8,128)S(1)} %copy.41, f32[32,256]{1,0:T(8,128)S(1)} %copy.42, f32[32,256]{1,0:T(8,128)S(1)} %copy.43), kind=kLoop, calls=%fused_computation.3.clone.1 | loop fusion | flops 3670016 | bytes 10551296 | tf_op jit(solution)/shard_map/while/body/eval_jaxpr/mul | solution.py:53
  85.1 0.1 fusion.54
  85.3 2.0 multiply_add_fusion.2
  87.2 2.4 %add.133 = f32[256,256]{1,0:T(8,128)S(1)} reshape(f32[16,16,16,16]{3,2,1,0:T(8,128)} %get-tuple-element.192) | data formatting | bytes 524288 | tf_op jit(solution)/shard_map/while/body/eval_jaxpr/add | solution.py:31
  89.7 0.9 sub.43
  90.7 9.8 %fusion.57 = f32[2048,512]{1,0:T(8,128)} fusion(f32[2048,256]{1,0:T(8,128)} %get-tuple-element.193, f32[2048,256]{1,0:T(8,128)} %get-tuple-element.194, f32[256,256]{0,1:T(8,128)S(1)} %bitcast.82, f32[256,256]{0,1:T(8,128)S(1)} %bitcast_negate_fusion.2, f32[256,256]{0,1:T(8,128)S(1)} %bitcast.80), kind=kOutput, calls=%fused_computation.8.clone.1 | convolution fusion | flops 6444285952 | bytes 9175040 | tf_op jit(solution)/shard_map/while/body/eval_jaxpr/dot_general | solution.py:54
  100.5 0.1 broadcast_in_dim.33
  100.5 0.1 reshape.240
  100.6 0.1 tile.19
  100.7 4.4 %fusion.58 = f32[2048,3]{0,1:T(4,128)S(1)} fusion(f32[2048,512]{1,0:T(8,128)} %fusion.57, f32[256,1]{0,1:T(1,128)S(1)} %tile.19, f32[256,1]{0,1:T(1,128)S(1)} %reshape.240, f32[3]{0:T(128)S(1)} %pad.6.clone.2), kind=kOutput, calls=%fused_computation.16.clone.1 | convolution fusion | flops 20448768 | bytes 4220940 | tf_op jit(solution)/shard_map/while/body/eval_jaxpr/dot_general | solution.py:56
  105.1 8.5 %fusion.55 = f32[2048,512]{1,0:T(8,128)S(1)} fusion(f32[2048,256]{1,0:T(8,128)} %get-tuple-element.187, f32[2048,256]{1,0:T(8,128)S(1)} %copy-done, f32[256,256]{0,1:T(8,128)S(1)} %bitcast.83, f32[256,256]{0,1:T(8,128)S(1)} %bitcast_negate_fusion.2, f32[256,256]{0,1:T(8,128)S(1)} %bitcast.81), kind=kOutput, calls=%fused_computation.4.clone.1 | convolution fusion | flops 6444285952 | bytes 9175040 | tf_op jit(solution)/shard_map/while/body/eval_jaxpr/dot_general | solution.py:54
  113.6 2.0 fusion.56
  115.7 0.1 fusion.59
  115.8 0.1 stack.28
  115.8 0.1 stack.29
  115.9 0.1 stack.30
  116.0 0.1 stack.31
  116.1 0.1 copy.44
  116.2 0.2 dynamic_update_slice.8
  116.5 9.7 %constant_dynamic-slice_fusion.2 = f32[1,64,32,16,16]{1,0,4,3,2:T(1,128)} fusion(f32[2,64,32,16,16]{1,0,4,3,2:T(2,128)} %get-tuple-element.223, s32[]{:T(128)} %get-tuple-element.209), kind=kLoop, calls=%fused_computation.46.clone.1 | loop fusion | bytes 4194308 | tf_op jit(solution)/shard_map/while/body/jit(dynamic_index_in_dim)/dynamic_slice | solution.py:94
  126.2 12.3 %copy.40 = f32[1,64,32,16,16]{2,1,4,3,0:T(8,128)} copy(f32[1,64,32,16,16]{1,0,4,3,2:T(1,128)} %constant_dynamic-slice_fusion.2) | data formatting | bytes 4194304 | tf_op jit(solution)/shard_map/while/body/jit(dynamic_index_in_dim)/dynamic_slice | solution.py:94
  138.5 7.5 %reshape.239 = f32[2048,256]{0,1:T(8,128)} reshape(f32[1,64,32,16,16]{2,1,4,3,0:T(8,128)} %copy.40) | data formatting | bytes 4194304 | tf_op jit(solution)/shard_map/while/body/eval_jaxpr/reshape | solution.py:47
  146.0 1.9 copy.41
  148.0 0.1 copy.43
  148.1 16.6 %bitcast_multiply_fusion.5 = (f32[2048,256]{1,0:T(8,128)}, f32[2048,256]{1,0:T(8,128)}, f32[2048,256]{1,0:T(8,128)}, f32[2048,256]{1,0:T(8,128)}) fusion(f32[2048,256]{1,0:T(8,128)S(1)} %copy.41, f32[32,256]{1,0:T(8,128)S(1)} %copy.42, f32[32,256]{1,0:T(8,128)S(1)} %copy.43), kind=kLoop, calls=%fused_computation.3.clone.1 | loop fusion | flops 3670016 | bytes 10551296 | tf_op jit(solution)/shard_map/while/body/eval_jaxpr/mul | solution.py:53
  164.7 0.1 fusion.54
  164.8 2.0 multiply_add_fusion.2
  166.8 2.4 %add.133 = f32[256,256]{1,0:T(8,128)S(1)} reshape(f32[16,16,16,16]{3,2,1,0:T(8,128)} %get-tuple-element.192) | data formatting | bytes 524288 | tf_op jit(solution)/shard_map/while/body/eval_jaxpr/add | solution.py:31
  169.3 0.9 sub.43
  170.2 9.8 %fusion.57 = f32[2048,512]{1,0:T(8,128)} fusion(f32[2048,256]{1,0:T(8,128)} %get-tuple-element.193, f32[2048,256]{1,0:T(8,128)} %get-tuple-element.194, f32[256,256]{0,1:T(8,128)S(1)} %bitcast.82, f32[256,256]{0,1:T(8,128)S(1)} %bitcast_negate_fusion.2, f32[256,256]{0,1:T(8,128)S(1)} %bitcast.80), kind=kOutput, calls=%fused_computation.8.clone.1 | convolution fusion | flops 6444285952 | bytes 9175040 | tf_op jit(solution)/shard_map/while/body/eval_jaxpr/dot_general | solution.py:54
  180.0 0.1 broadcast_in_dim.33
  180.1 0.1 reshape.240
  180.2 0.1 tile.19
  180.3 4.4 %fusion.58 = f32[2048,3]{0,1:T(4,128)S(1)} fusion(f32[2048,512]{1,0:T(8,128)} %fusion.57, f32[256,1]{0,1:T(1,128)S(1)} %tile.19, f32[256,1]{0,1:T(1,128)S(1)} %reshape.240, f32[3]{0:T(128)S(1)} %pad.6.clone.2), kind=kOutput, calls=%fused_computation.16.clone.1 | convolution fusion | flops 20448768 | bytes 4220940 | tf_op jit(solution)/shard_map/while/body/eval_jaxpr/dot_general | solution.py:56
  184.7 8.5 %fusion.55 = f32[2048,512]{1,0:T(8,128)S(1)} fusion(f32[2048,256]{1,0:T(8,128)} %get-tuple-element.187, f32[2048,256]{1,0:T(8,128)S(1)} %copy-done, f32[256,256]{0,1:T(8,128)S(1)} %bitcast.83, f32[256,256]{0,1:T(8,128)S(1)} %bitcast_negate_fusion.2, f32[256,256]{0,1:T(8,128)S(1)} %bitcast.81), kind=kOutput, calls=%fused_computation.4.clone.1 | convolution fusion | flops 6444285952 | bytes 9175040 | tf_op jit(solution)/shard_map/while/body/eval_jaxpr/dot_general | solution.py:54
  193.2 2.0 fusion.56
  195.2 0.1 fusion.59
  195.3 0.1 stack.28
  195.4 0.1 stack.29
  195.6 0.1 stack.31
  195.7 0.1 copy.44
  195.8 0.2 dynamic_update_slice.8
  196.0 0.1 reshape.212
  196.1 39.6 %all_gather.3 = bf16[128,2,512]{0,2,1:T(8,128)(2,1)S(1)} all-gather(bf16[128,2,32]{0,2,1:T(8,128)(2,1)S(1)} %reshape.212), channel_id=1, replica_groups=mesh['group'=2,'tile'=16] {'tile'}, dimensions={2}, use_global_device_ids=true | all-gather | bytes 278528 | tf_op jit(solution)/shard_map/all_gather | solution.py:99
  235.7 0.3 fusion.30
  236.0 0.9 copy.31
  (38 shorter events, 0.4 us)
Async XLA Ops:
  0.0 7.7 %copy-start.3 = (s32[128,72]{0,1:T(8,128)S(1)}, s32[128,72]{0,1:T(8,128)}, u32[]{:S(2)}) copy-start(s32[128,72]{0,1:T(8,128)} %param.8) | copy-start | bytes 110596
  0.0 7.7 %copy-start.4 = (f32[72]{0:T(128)S(1)}, f32[72]{0:T(128)}, u32[]{:S(2)}) copy-start(f32[72]{0:T(128)} %param.9) | copy-start | bytes 868
  2.8 12.4 %copy-start.5 = (s32[32]{0:T(128)S(1)}, s32[32]{0:T(128)}, u32[]{:S(2)}) copy-start(s32[32]{0:T(128)} %param.13) | copy-start | bytes 388
  2.8 12.4 %collective-permute-start.1 = (bf16[72,8192]{1,0:T(8,128)(2,1)}, bf16[72,8192]{1,0:T(8,128)(2,1)}, u32[]{:S(2)}, u32[]{:S(2)}) collective-permute-start(bf16[72,8192]{1,0:T(8,128)(2,1)} %get-tuple-element.136), channel_id=1, source_target_pairs={{0,1},{1,2},{2,3},{3,4},{4,5},{5,6},{6,7},{7,8},{8,9},{9,10},{10,1... | collective-permute-start | bytes 3538952 | tf_op jit(solution)/shard_map/ppermute | solution.py:14
  6.4 10.9 %collective-permute-start.3 = (bf16[72,8192]{1,0:T(8,128)(2,1)S(1)}, bf16[72,8192]{1,0:T(8,128)(2,1)}, u32[]{:S(2)}, u32[]{:S(2)}) collective-permute-start(bf16[72,8192]{1,0:T(8,128)(2,1)S(1)} %get-tuple-element.137), channel_id=1, source_target_pairs={{1,0},{2,1},{3,2},{4,3},{5,4},{6,5},{7,6},{8,7},{9,8},{10,9},{11,1... | collective-permute-start | bytes 3538952 | tf_op jit(solution)/shard_map/ppermute | solution.py:14
  7.8 7.5 %collective-permute-start = (bf16[128,72]{0,1:T(8,128)(2,1)S(1)}, bf16[128,72]{0,1:T(8,128)(2,1)S(1)}, u32[]{:S(2)}, u32[]{:S(2)}) collective-permute-start(bf16[128,72]{0,1:T(8,128)(2,1)S(1)} %multiply_convert_fusion), channel_id=1, source_target_pairs={{0,1},{1,2},{2,3},{3,4},{4,5},{5,6},{6,7},{7,8},{8,9},{9,10},{10,1... | collective-permute-start | bytes 55304 | tf_op jit(solution)/shard_map/ppermute | solution.py:14
  11.9 5.4 %collective-permute-start.2 = (bf16[128,72]{0,1:T(8,128)(2,1)S(1)}, bf16[128,72]{0,1:T(8,128)(2,1)S(1)}, u32[]{:S(2)}, u32[]{:S(2)}) collective-permute-start(bf16[128,72]{0,1:T(8,128)(2,1)S(1)} %multiply_convert_fusion), channel_id=1, source_target_pairs={{1,0},{2,1},{3,2},{4,3},{5,4},{6,5},{7,6},{8,7},{9,8},{10,9},{11,1... | collective-permute-start | bytes 55304 | tf_op jit(solution)/shard_map/ppermute | solution.py:14
  27.7 9.2 %copy-start.1 = (f32[32,16,16]{0,2,1:T(8,128)S(1)}, f32[32,16,16]{0,2,1:T(8,128)}, u32[]{:S(2)}) copy-start(f32[32,16,16]{0,2,1:T(8,128)} %param.11) | copy-start | bytes 98308
  27.7 9.2 %copy-start.2 = (f32[32,16,16]{0,2,1:T(8,128)S(1)}, f32[32,16,16]{0,2,1:T(8,128)}, u32[]{:S(2)}) copy-start(f32[32,16,16]{0,2,1:T(8,128)} %param.12) | copy-start | bytes 98308
  100.5 4.7 %copy-start = (f32[2048,256]{1,0:T(8,128)S(1)}, f32[2048,256]{1,0:T(8,128)}, u32[]{:S(2)}) copy-start(f32[2048,256]{1,0:T(8,128)} %get-tuple-element.188) | copy-start | bytes 6291460 | tf_op jit(solution)/shard_map/while
  180.0 4.7 %copy-start = (f32[2048,256]{1,0:T(8,128)S(1)}, f32[2048,256]{1,0:T(8,128)}, u32[]{:S(2)}) copy-start(f32[2048,256]{1,0:T(8,128)} %get-tuple-element.188) | copy-start | bytes 6291460 | tf_op jit(solution)/shard_map/while
where the time goes:
time: 238 us; the launch traced here: 237 us
  local copies, waits for them, and re-layouts  90.3 us (38%)
  matrix products  55.7 us (23%)
  other arithmetic  40.7 us (17%)
  blocking collectives  39.6 us (17%)
  starting transfers between devices  10.3 us (4%)
    dynamic_slice x4, local copies, waits for them, and re-layouts, per_device(): slopes = lax.map(one_block, blocks).reshape(patterns, 2, sub_count)  44.1 us
    all_gather x1, blocking collectives, per_device(): lax.all_gather(shortened(slopes), 'tile', axis=2, tiled=True)  39.6 us
    dot_general x4, matrix products, spot_slopes(): jnp.dot(field.reshape(patterns * sub_count, 2 * flat), transform, precisi...  36.6 us
    mul x2, other arithmetic, spot_slopes(): amp_rows * jnp.cos(angles)  33.3 us
    reshape x4, local copies, waits for them, and re-layouts, spot_slopes(): phase_rows = phase_map.reshape(patterns, sub_count, flat)  18.8 us
    dot_general x4, matrix products, spot_slopes(): sums = jnp.dot(intensity, moments, precision=HIGHEST)  12.9 us
    ppermute x4, starting transfers between devices, passed_along(): lax.ppermute(value, axis, [(source, source + steps) for source in range(f...  10.3 us
    reshape x1, local copies, waits for them, and re-layouts, per_device(): phase_map.reshape(patterns // block_rows, block_rows, sub_count, samples,...  9.2 us
  transfers between devices with their start and end apart: 4, of which 0 were waited for; matrix products, arithmetic and copies ran while one was open for 2% of the time, Pallas kernels for 0%

commit v1 on v0

--- a/solution.py
+++ b/solution.py
@@ -6,6 +6,23 @@
 
 PIX = 16
 HIGHEST = lax.Precision.HIGHEST
+
+
+def fix_tasks_over_axis(shard_in, row_dim):
+    top, k_now = (jax.lax.axis_size("tile"), jax.lax.axis_index("tile"))
+    f_next, x_now = (shard_in, 1)
+    while x_now < top:
+        column = []
+        q = 0
+        while q < top:
+            column.append((q, q ^ x_now))
+            q = q + 1
+        mat_out = jax.lax.ppermute(f_next, "tile", column)
+        low = jnp.concatenate([f_next, mat_out], row_dim)
+        front = jnp.concatenate([mat_out, f_next], row_dim)
+        f_next = jnp.where(k_now & x_now == 0, low, front)
+        x_now = 2 * x_now
+    return f_next
 
 
 def passed_along(value, axis, steps):
@@ -96,7 +113,7 @@
     summed = jnp.einsum(
         "pa,pcs->acs",
         signs_half,
-        lax.all_gather(shortened(slopes), "tile", axis=2, tiled=True),
+        fix_tasks_over_axis(shortened(slopes), row_dim=2),
         preferred_element_type=jnp.float32,
     )
     return summed / (patterns * stroke)[:, None, None]

time: 238 us -> 235 us (0.987)
  blocking collectives: 39.6 us -> 0 us
  starting transfers between devices: 10.3 us -> 36.5 us
  waiting for transfers between devices: 0.01 us -> 10.1 us
    all_gather x1 -> x0, blocking collectives: 39.6 us -> none  [per_device(): lax.all_gather(shortened(slopes), 'tile', axis=2, tiled=True)]
    ppermute x0 -> x4, starting transfers between devices: none -> 26.2 us  [fix_tasks_over_axis(): mat_out = jax.lax.ppermute(f_next, 'tile', column)]
    ppermute x0 -> x4, waiting for transfers between devices: none -> 10.1 us  [fix_tasks_over_axis(): mat_out = jax.lax.ppermute(f_next, 'tile', column)]
  transfers between devices with their start and end apart: 4 -> 8, of which waited for: 0 -> 4; matrix products, arithmetic and copies ran while one was open for 2% -> 2% of each run, Pallas kernels for 0% -> 0%
where the time goes in v1:
time: 235 us; the launch traced here: 234 us
  local copies, waits for them, and re-layouts  90.3 us (38%)
  matrix products  55.8 us (24%)
  other arithmetic  40.8 us (17%)
  starting transfers between devices  36.5 us (16%)
  waiting for transfers between devices  10.1 us (4%)
    dynamic_slice x4, local copies, waits for them, and re-layouts, per_device(): slopes = lax.map(one_block, blocks).reshape(patterns, 2, sub_count)  44.1 us
    dot_general x4, matrix products, spot_slopes(): jnp.dot(field.reshape(patterns * sub_count, 2 * flat), transform, precisi...  36.6 us
    mul x2, other arithmetic, spot_slopes(): amp_rows * jnp.cos(angles)  33.2 us
    ppermute x4, starting transfers between devices, fix_tasks_over_axis(): mat_out = jax.lax.ppermute(f_next, 'tile', column)  26.2 us
    reshape x4, local copies, waits for them, and re-layouts, spot_slopes(): phase_rows = phase_map.reshape(patterns, sub_count, flat)  18.8 us
    dot_general x4, matrix products, spot_slopes(): sums = jnp.dot(intensity, moments, precision=HIGHEST)  12.9 us
    ppermute x4, starting transfers between devices, passed_along(): lax.ppermute(value, axis, [(source, source + steps) for source in range(f...  10.3 us
    ppermute x4, waiting for transfers between devices, fix_tasks_over_axis(): mat_out = jax.lax.ppermute(f_next, 'tile', column)  10.1 us
  transfers between devices with their start and end apart: 8, of which 4 were waited for; matrix products, arithmetic and copies ran while one was open for 2% of the time, Pallas kernels for 0%

profile of v1, /device:TPU:0, one launch (start us, length us, event | category | flops | bytes accessed | tf_op | source)
XLA Modules:
  0.0 233.8 jit_solution(15763440504330136849)
XLA Ops:
  0.0 2.9 %slice_bitcast_fusion.1 = (bf16[72,8192]{1,0:T(8,128)(2,1)}, bf16[72,8192]{1,0:T(8,128)(2,1)S(1)}) fusion(bf16[3,72,8192]{2,1,0:T(8,128)(2,1)} %param.10), kind=kLoop, calls=%fused_computation.58 | loop fusion | bytes 4718592 | tf_op jit(solution)/shard_map/squeeze | solution.py:96
  2.9 3.6 %collective-permute-start.1 = (bf16[72,8192]{1,0:T(8,128)(2,1)}, bf16[72,8192]{1,0:T(8,128)(2,1)}, u32[]{:S(2)}, u32[]{:S(2)}) collective-permute-start(bf16[72,8192]{1,0:T(8,128)(2,1)} %get-tuple-element.136), channel_id=1, source_target_pairs={{0,1},{1,2},{2,3},{3,4},{4,5},{5,6},{6,7},{7,8},{8,9},{9,10},{10,1... | collective-permute-start | bytes 3538952 | tf_op jit(solution)/shard_map/ppermute | solution.py:31
  6.4 1.3 collective-permute-start.3
  7.7 0.1 multiply_convert_fusion
  7.8 4.1 %collective-permute-start = (bf16[128,72]{0,1:T(8,128)(2,1)S(1)}, bf16[128,72]{0,1:T(8,128)(2,1)S(1)}, u32[]{:S(2)}, u32[]{:S(2)}) collective-permute-start(bf16[128,72]{0,1:T(8,128)(2,1)S(1)} %multiply_convert_fusion), channel_id=1, source_target_pairs={{0,1},{1,2},{2,3},{3,4},{4,5},{5,6},{6,7},{7,8},{8,9},{9,10},{10,1... | collective-permute-start | bytes 55304 | tf_op jit(solution)/shard_map/ppermute | solution.py:31
  11.9 1.3 collective-permute-start.2
  13.2 2.0 convolution_convert_fusion.2
  15.3 2.0 convolution_convert_fusion.1
  17.3 2.0 convolution_convert_fusion
  19.3 2.8 %convert_add_fusion = f32[128,8192]{1,0:T(8,128)} fusion(bf16[128,8192]{1,0:T(8,128)(2,1)S(1)} %convolution_convert_fusion, bf16[128,8192]{1,0:T(8,128)(2,1)S(1)} %convolution_convert_fusion.1, bf16[128,8192]{1,0:T(8,128)(2,1)S(1)} %convolution_convert_fusion.2), kind=kLoop, calls=%fused_computation.55 | loop fusion | flops 5242880 | bytes 10485760 | tf_op jit(solution)/shard_map/add | solution.py:101
  22.1 5.6 %copy.29 = f32[128,8192]{0,1:T(8,128)} copy(f32[128,8192]{1,0:T(8,128)} %convert_add_fusion) | data formatting | bytes 8388608 | tf_op jit(solution)/shard_map/add | solution.py:101
  27.7 9.2 %reshape.211 = f32[2,64,32,16,16]{1,0,4,3,2:T(2,128)} reshape(f32[128,8192]{0,1:T(8,128)} %copy.29) | data formatting | bytes 8388608 | tf_op jit(solution)/shard_map/reshape | solution.py:106
  36.9 159.1 %while.12 = (s32[]{:T(128)}, bf16[2,64,2,32]{1,0,3,2:T(2,128)(2,1)S(1)}, f32[32,16,16]{0,2,1:T(8,128)S(1)}, f32[32,16,16]{0,2,1:T(8,128)S(1)}, f32[2,64,32,16,16...) while((s32[]{:T(128)}, ...), condition=%wide.region_1.2_spmd, body=%wide.region_0.1_spmd.sunk | while | flops 12933627904 | bytes 64969588 | solution.py:111
  36.9 9.7 %constant_dynamic-slice_fusion.2 = f32[1,64,32,16,16]{1,0,4,3,2:T(1,128)} fusion(f32[2,64,32,16,16]{1,0,4,3,2:T(2,128)} %get-tuple-element.223, s32[]{:T(128)} %get-tuple-element.209), kind=kLoop, calls=%fused_computation.46.clone.1 | loop fusion | bytes 4194308 | tf_op jit(solution)/shard_map/while/body/jit(dynamic_index_in_dim)/dynamic_slice | solution.py:111
  46.7 12.3 %copy.43 = f32[1,64,32,16,16]{2,1,4,3,0:T(8,128)} copy(f32[1,64,32,16,16]{1,0,4,3,2:T(1,128)} %constant_dynamic-slice_fusion.2) | data formatting | bytes 4194304 | tf_op jit(solution)/shard_map/while/body/jit(dynamic_index_in_dim)/dynamic_slice | solution.py:111
  59.0 7.5 %reshape.239 = f32[2048,256]{0,1:T(8,128)} reshape(f32[1,64,32,16,16]{2,1,4,3,0:T(8,128)} %copy.43) | data formatting | bytes 4194304 | tf_op jit(solution)/shard_map/while/body/eval_jaxpr/reshape | solution.py:64
  66.5 1.9 copy.44
  68.4 0.1 copy.46
  68.5 16.6 %bitcast_multiply_fusion.5 = (f32[2048,256]{1,0:T(8,128)}, f32[2048,256]{1,0:T(8,128)}, f32[2048,256]{1,0:T(8,128)}, f32[2048,256]{1,0:T(8,128)}) fusion(f32[2048,256]{1,0:T(8,128)S(1)} %copy.44, f32[32,256]{1,0:T(8,128)S(1)} %copy.45, f32[32,256]{1,0:T(8,128)S(1)} %copy.46), kind=kLoop, calls=%fused_computation.3.clone.1 | loop fusion | flops 3670016 | bytes 10551296 | tf_op jit(solution)/shard_map/while/body/eval_jaxpr/mul | solution.py:70
  85.1 0.1 fusion.60
  85.3 2.0 multiply_add_fusion.2
  87.3 2.4 %add.133 = f32[256,256]{1,0:T(8,128)S(1)} reshape(f32[16,16,16,16]{3,2,1,0:T(8,128)} %get-tuple-element.192) | data formatting | bytes 524288 | tf_op jit(solution)/shard_map/while/body/eval_jaxpr/add | solution.py:48
  89.7 0.9 sub.43
  90.7 9.8 %fusion.63 = f32[2048,512]{1,0:T(8,128)} fusion(f32[2048,256]{1,0:T(8,128)} %get-tuple-element.193, f32[2048,256]{1,0:T(8,128)} %get-tuple-element.194, f32[256,256]{0,1:T(8,128)S(1)} %bitcast.81, f32[256,256]{0,1:T(8,128)S(1)} %bitcast_negate_fusion.2, f32[256,256]{0,1:T(8,128)S(1)} %bitcast.79), kind=kOutput, calls=%fused_computation.8.clone.1 | convolution fusion | flops 6444285952 | bytes 9175040 | tf_op jit(solution)/shard_map/while/body/eval_jaxpr/dot_general | solution.py:71
  100.5 0.1 broadcast_in_dim.33
  100.6 0.1 reshape.240
  100.7 0.1 tile.19
  100.8 4.4 %fusion.64 = f32[2048,3]{0,1:T(4,128)S(1)} fusion(f32[2048,512]{1,0:T(8,128)} %fusion.63, f32[256,1]{0,1:T(1,128)S(1)} %tile.19, f32[256,1]{0,1:T(1,128)S(1)} %reshape.240, f32[3]{0:T(128)S(1)} %pad.6.clone.2), kind=kOutput, calls=%fused_computation.16.clone.1 | convolution fusion | flops 20448768 | bytes 4220940 | tf_op jit(solution)/shard_map/while/body/eval_jaxpr/dot_general | solution.py:73
  105.1 8.5 %fusion.61 = f32[2048,512]{1,0:T(8,128)S(1)} fusion(f32[2048,256]{1,0:T(8,128)} %get-tuple-element.187, f32[2048,256]{1,0:T(8,128)S(1)} %copy-done, f32[256,256]{0,1:T(8,128)S(1)} %bitcast.82, f32[256,256]{0,1:T(8,128)S(1)} %bitcast_negate_fusion.2, f32[256,256]{0,1:T(8,128)S(1)} %bitcast.80), kind=kOutput, calls=%fused_computation.4.clone.1 | convolution fusion | flops 6444285952 | bytes 9175040 | tf_op jit(solution)/shard_map/while/body/eval_jaxpr/dot_general | solution.py:71
  113.6 2.0 fusion.62
  115.7 0.1 fusion.65
  116.1 0.1 copy.47
  116.2 0.2 dynamic_update_slice.8
  116.5 9.7 %constant_dynamic-slice_fusion.2 = f32[1,64,32,16,16]{1,0,4,3,2:T(1,128)} fusion(f32[2,64,32,16,16]{1,0,4,3,2:T(2,128)} %get-tuple-element.223, s32[]{:T(128)} %get-tuple-element.209), kind=kLoop, calls=%fused_computation.46.clone.1 | loop fusion | bytes 4194308 | tf_op jit(solution)/shard_map/while/body/jit(dynamic_index_in_dim)/dynamic_slice | solution.py:111
  126.2 12.3 %copy.43 = f32[1,64,32,16,16]{2,1,4,3,0:T(8,128)} copy(f32[1,64,32,16,16]{1,0,4,3,2:T(1,128)} %constant_dynamic-slice_fusion.2) | data formatting | bytes 4194304 | tf_op jit(solution)/shard_map/while/body/jit(dynamic_index_in_dim)/dynamic_slice | solution.py:111
  138.5 7.5 %reshape.239 = f32[2048,256]{0,1:T(8,128)} reshape(f32[1,64,32,16,16]{2,1,4,3,0:T(8,128)} %copy.43) | data formatting | bytes 4194304 | tf_op jit(solution)/shard_map/while/body/eval_jaxpr/reshape | solution.py:64
  146.0 1.9 copy.44
  148.0 0.1 copy.46
  148.1 16.6 %bitcast_multiply_fusion.5 = (f32[2048,256]{1,0:T(8,128)}, f32[2048,256]{1,0:T(8,128)}, f32[2048,256]{1,0:T(8,128)}, f32[2048,256]{1,0:T(8,128)}) fusion(f32[2048,256]{1,0:T(8,128)S(1)} %copy.44, f32[32,256]{1,0:T(8,128)S(1)} %copy.45, f32[32,256]{1,0:T(8,128)S(1)} %copy.46), kind=kLoop, calls=%fused_computation.3.clone.1 | loop fusion | flops 3670016 | bytes 10551296 | tf_op jit(solution)/shard_map/while/body/eval_jaxpr/mul | solution.py:70
  164.7 0.1 fusion.60
  164.8 2.0 multiply_add_fusion.2
  166.8 2.4 %add.133 = f32[256,256]{1,0:T(8,128)S(1)} reshape(f32[16,16,16,16]{3,2,1,0:T(8,128)} %get-tuple-element.192) | data formatting | bytes 524288 | tf_op jit(solution)/shard_map/while/body/eval_jaxpr/add | solution.py:48
  169.3 0.9 sub.43
  170.2 9.8 %fusion.63 = f32[2048,512]{1,0:T(8,128)} fusion(f32[2048,256]{1,0:T(8,128)} %get-tuple-element.193, f32[2048,256]{1,0:T(8,128)} %get-tuple-element.194, f32[256,256]{0,1:T(8,128)S(1)} %bitcast.81, f32[256,256]{0,1:T(8,128)S(1)} %bitcast_negate_fusion.2, f32[256,256]{0,1:T(8,128)S(1)} %bitcast.79), kind=kOutput, calls=%fused_computation.8.clone.1 | convolution fusion | flops 6444285952 | bytes 9175040 | tf_op jit(solution)/shard_map/while/body/eval_jaxpr/dot_general | solution.py:71
  180.1 0.1 broadcast_in_dim.33
  180.1 0.1 reshape.240
  180.2 0.1 tile.19
  180.3 4.4 %fusion.64 = f32[2048,3]{0,1:T(4,128)S(1)} fusion(f32[2048,512]{1,0:T(8,128)} %fusion.63, f32[256,1]{0,1:T(1,128)S(1)} %tile.19, f32[256,1]{0,1:T(1,128)S(1)} %reshape.240, f32[3]{0:T(128)S(1)} %pad.6.clone.2), kind=kOutput, calls=%fused_computation.16.clone.1 | convolution fusion | flops 20448768 | bytes 4220940 | tf_op jit(solution)/shard_map/while/body/eval_jaxpr/dot_general | solution.py:73
  184.7 8.5 %fusion.61 = f32[2048,512]{1,0:T(8,128)S(1)} fusion(f32[2048,256]{1,0:T(8,128)} %get-tuple-element.187, f32[2048,256]{1,0:T(8,128)S(1)} %copy-done, f32[256,256]{0,1:T(8,128)S(1)} %bitcast.82, f32[256,256]{0,1:T(8,128)S(1)} %bitcast_negate_fusion.2, f32[256,256]{0,1:T(8,128)S(1)} %bitcast.80), kind=kOutput, calls=%fused_computation.4.clone.1 | convolution fusion | flops 6444285952 | bytes 9175040 | tf_op jit(solution)/shard_map/while/body/eval_jaxpr/dot_general | solution.py:71
  193.2 2.0 fusion.62
  195.2 0.1 fusion.65
  195.7 0.1 copy.47
  195.8 0.2 dynamic_update_slice.8
  196.0 0.1 reshape.212
  196.1 19.1 %collective-permute-start.4 = (bf16[128,2,32]{0,2,1:T(8,128)(2,1)S(1)}, bf16[128,2,32]{0,2,1:T(8,128)(2,1)S(1)}, u32[]{:S(2)}, u32[]{:S(2)}) collective-permute-start(bf16[128,2,32]{0,2,1:T(8,128)(2,1)S(1)} %reshape.212), channel_id=1, source_target_pairs={{0,1},{1,0},{2,3},{3,2},{4,5},{5,4},{6,7},{7,6},{8,9},{9,8},{10,11... | collective-permute-start | bytes 49160 | tf_op jit(solution)/shard_map/ppermute | solution.py:20
  215.3 0.8 collective-permute-done.4
  216.1 2.8 %collective-permute-start.5 = (bf16[128,2,64]{0,2,1:T(8,128)(2,1)S(1)}, bf16[128,2,64]{0,2,1:T(8,128)(2,1)S(1)}, u32[]{:S(2)}, u32[]{:S(2)}) collective-permute-start(bf16[128,2,64]{0,2,1:T(8,128)(2,1)S(1)} %maximum_select_fusion.4), channel_id=1, source_target_pairs={{0,2},{1,3},{2,0},{3,1},{4,6},{5,7},{6,4},{7,5},{8,10},{9,11},{10,... | collective-permute-start | bytes 98312 | tf_op jit(solution)/shard_map/ppermute | solution.py:20
  218.9 1.9 collective-permute-done.5
  220.8 1.6 collective-permute-start.6
  222.5 2.7 %collective-permute-done.6 = bf16[128,2,128]{0,2,1:T(8,128)(2,1)S(1)} collective-permute-done((bf16[128,2,128]{0,2,1:T(8,128)(2,1)S(1)}, bf16[128,2,128]{0,2,1:T(8,128)(2,1)S(1)}, u32[]{:S(2)}, u32[]{:S(2)}) %collective-permute-start.6) | collective-permute-done | bytes 65568 | tf_op jit(solution)/shard_map/ppermute | solution.py:20
  225.2 2.7 %collective-permute-start.7 = (bf16[128,2,256]{0,2,1:T(8,128)(2,1)S(1)}, bf16[128,2,256]{0,2,1:T(8,128)(2,1)S(1)}, u32[]{:S(2)}, u32[]{:S(2)}) collective-permute-start(bf16[128,2,256]{0,2,1:T(8,128)(2,1)S(1)} %maximum_select_fusion.2), channel_id=1, source_target_pairs={{0,8},{1,9},{2,10},{3,11},{4,12},{5,13},{6,14},{7,15},{8,0},{9,1},... | collective-permute-start | bytes 393224 | tf_op jit(solution)/shard_map/ppermute | solution.py:20
  227.9 4.7 %collective-permute-done.7 = bf16[128,2,256]{0,2,1:T(8,128)(2,1)S(1)} collective-permute-done((bf16[128,2,256]{0,2,1:T(8,128)(2,1)S(1)}, bf16[128,2,256]{0,2,1:T(8,128)(2,1)S(1)}, u32[]{:S(2)}, u32[]{:S(2)}) %collective-permute-start.7) | collective-permute-done | bytes 131104 | tf_op jit(solution)/shard_map/ppermute | solution.py:20
  232.5 0.3 fusion.30
  232.8 0.9 copy.33
  (48 shorter events, 0.9 us)
Async XLA Ops:
  0.0 7.7 %copy-start.3 = (s32[128,72]{0,1:T(8,128)S(1)}, s32[128,72]{0,1:T(8,128)}, u32[]{:S(2)}) copy-start(s32[128,72]{0,1:T(8,128)} %param.8) | copy-start | bytes 110596
  0.0 7.7 %copy-start.4 = (f32[72]{0:T(128)S(1)}, f32[72]{0:T(128)}, u32[]{:S(2)}) copy-start(f32[72]{0:T(128)} %param.9) | copy-start | bytes 868
  2.9 12.4 %copy-start.5 = (s32[32]{0:T(128)S(1)}, s32[32]{0:T(128)}, u32[]{:S(2)}) copy-start(s32[32]{0:T(128)} %param.13) | copy-start | bytes 388
  2.9 12.4 %collective-permute-start.1 = (bf16[72,8192]{1,0:T(8,128)(2,1)}, bf16[72,8192]{1,0:T(8,128)(2,1)}, u32[]{:S(2)}, u32[]{:S(2)}) collective-permute-start(bf16[72,8192]{1,0:T(8,128)(2,1)} %get-tuple-element.136), channel_id=1, source_target_pairs={{0,1},{1,2},{2,3},{3,4},{4,5},{5,6},{6,7},{7,8},{8,9},{9,10},{10,1... | collective-permute-start | bytes 3538952 | tf_op jit(solution)/shard_map/ppermute | solution.py:31
  6.4 10.9 %collective-permute-start.3 = (bf16[72,8192]{1,0:T(8,128)(2,1)S(1)}, bf16[72,8192]{1,0:T(8,128)(2,1)}, u32[]{:S(2)}, u32[]{:S(2)}) collective-permute-start(bf16[72,8192]{1,0:T(8,128)(2,1)S(1)} %get-tuple-element.137), channel_id=1, source_target_pairs={{1,0},{2,1},{3,2},{4,3},{5,4},{6,5},{7,6},{8,7},{9,8},{10,9},{11,1... | collective-permute-start | bytes 3538952 | tf_op jit(solution)/shard_map/ppermute | solution.py:31
  7.8 7.5 %collective-permute-start = (bf16[128,72]{0,1:T(8,128)(2,1)S(1)}, bf16[128,72]{0,1:T(8,128)(2,1)S(1)}, u32[]{:S(2)}, u32[]{:S(2)}) collective-permute-start(bf16[128,72]{0,1:T(8,128)(2,1)S(1)} %multiply_convert_fusion), channel_id=1, source_target_pairs={{0,1},{1,2},{2,3},{3,4},{4,5},{5,6},{6,7},{7,8},{8,9},{9,10},{10,1... | collective-permute-start | bytes 55304 | tf_op jit(solution)/shard_map/ppermute | solution.py:31
  11.9 5.4 %collective-permute-start.2 = (bf16[128,72]{0,1:T(8,128)(2,1)S(1)}, bf16[128,72]{0,1:T(8,128)(2,1)S(1)}, u32[]{:S(2)}, u32[]{:S(2)}) collective-permute-start(bf16[128,72]{0,1:T(8,128)(2,1)S(1)} %multiply_convert_fusion), channel_id=1, source_target_pairs={{1,0},{2,1},{3,2},{4,3},{5,4},{6,5},{7,6},{8,7},{9,8},{10,9},{11,1... | collective-permute-start | bytes 55304 | tf_op jit(solution)/shard_map/ppermute | solution.py:31
  27.7 9.2 %copy-start.1 = (f32[32,16,16]{0,2,1:T(8,128)S(1)}, f32[32,16,16]{0,2,1:T(8,128)}, u32[]{:S(2)}) copy-start(f32[32,16,16]{0,2,1:T(8,128)} %param.11) | copy-start | bytes 98308
  27.7 9.2 %copy-start.2 = (f32[32,16,16]{0,2,1:T(8,128)S(1)}, f32[32,16,16]{0,2,1:T(8,128)}, u32[]{:S(2)}) copy-start(f32[32,16,16]{0,2,1:T(8,128)} %param.12) | copy-start | bytes 98308
  100.5 4.7 %copy-start = (f32[2048,256]{1,0:T(8,128)S(1)}, f32[2048,256]{1,0:T(8,128)}, u32[]{:S(2)}) copy-start(f32[2048,256]{1,0:T(8,128)} %get-tuple-element.188) | copy-start | bytes 6291460 | tf_op jit(solution)/shard_map/while
  180.1 4.7 %copy-start = (f32[2048,256]{1,0:T(8,128)S(1)}, f32[2048,256]{1,0:T(8,128)}, u32[]{:S(2)}) copy-start(f32[2048,256]{1,0:T(8,128)} %get-tuple-element.188) | copy-start | bytes 6291460 | tf_op jit(solution)/shard_map/while
  196.1 20.0 %collective-permute-start.4 = (bf16[128,2,32]{0,2,1:T(8,128)(2,1)S(1)}, bf16[128,2,32]{0,2,1:T(8,128)(2,1)S(1)}, u32[]{:S(2)}, u32[]{:S(2)}) collective-permute-start(bf16[128,2,32]{0,2,1:T(8,128)(2,1)S(1)} %reshape.212), channel_id=1, source_target_pairs={{0,1},{1,0},{2,3},{3,2},{4,5},{5,4},{6,7},{7,6},{8,9},{9,8},{10,11... | collective-permute-start | bytes 49160 | tf_op jit(solution)/shard_map/ppermute | solution.py:20
  216.1 4.7 %collective-permute-start.5 = (bf16[128,2,64]{0,2,1:T(8,128)(2,1)S(1)}, bf16[128,2,64]{0,2,1:T(8,128)(2,1)S(1)}, u32[]{:S(2)}, u32[]{:S(2)}) collective-permute-start(bf16[128,2,64]{0,2,1:T(8,128)(2,1)S(1)} %maximum_select_fusion.4), channel_id=1, source_target_pairs={{0,2},{1,3},{2,0},{3,1},{4,6},{5,7},{6,4},{7,5},{8,10},{9,11},{10,... | collective-permute-start | bytes 98312 | tf_op jit(solution)/shard_map/ppermute | solution.py:20
  220.8 4.3 %collective-permute-start.6 = (bf16[128,2,128]{0,2,1:T(8,128)(2,1)S(1)}, bf16[128,2,128]{0,2,1:T(8,128)(2,1)S(1)}, u32[]{:S(2)}, u32[]{:S(2)}) collective-permute-start(bf16[128,2,128]{0,2,1:T(8,128)(2,1)S(1)} %maximum_select_fusion.3), channel_id=1, source_target_pairs={{0,4},{1,5},{2,6},{3,7},{4,0},{5,1},{6,2},{7,3},{8,12},{9,13},{10,... | collective-permute-start | bytes 196616 | tf_op jit(solution)/shard_map/ppermute | solution.py:20
  225.2 7.3 %collective-permute-start.7 = (bf16[128,2,256]{0,2,1:T(8,128)(2,1)S(1)}, bf16[128,2,256]{0,2,1:T(8,128)(2,1)S(1)}, u32[]{:S(2)}, u32[]{:S(2)}) collective-permute-start(bf16[128,2,256]{0,2,1:T(8,128)(2,1)S(1)} %maximum_select_fusion.2), channel_id=1, source_target_pairs={{0,8},{1,9},{2,10},{3,11},{4,12},{5,13},{6,14},{7,15},{8,0},{9,1},... | collective-permute-start | bytes 393224 | tf_op jit(solution)/shard_map/ppermute | solution.py:20
